TPU v7x, 32 devices: a whole 2x2x4 slice. The times are simulated.
32 devices in a mesh: groups: 2 (over y), expert: 8 (over z, x), mp: 2 (over core).
Axes of the slice: x: 2, y: 2, z: 4, core: 2. Of those that a mesh axis runs over, the one named last changes fastest.
Arguments:
- tokens: bfloat16 [64, 6144], P(('groups', 'expert', 'mp')), parts along dimension 0, may hold values from -6 to 6
- expert_ids: int32 [64, 2], P(('groups', 'expert', 'mp')), parts along dimension 0, may hold values from 0 to 3, all different within a row; in each aligned block of 2 rows (0 to 1, 2 to 3, ...) at most 2 rows name the same one
- mix_weights: float32 [64, 2], P(('groups', 'expert', 'mp')), parts along dimension 0, may hold values from 0.2 to 1
- w_gate: bfloat16 [6144, 32768], P(None, ('expert', 'mp')), may hold values from -0.078125 to 0.078125
- w_up: bfloat16 [6144, 32768], P(None, ('expert', 'mp')), may hold values from -0.078125 to 0.078125
- w_down: bfloat16 [32768, 6144], P(('expert', 'mp')), may hold values from -0.0625 to 0.0625
Outputs:
- combined: bfloat16 [64, 6144], P(('groups', 'expert', 'mp')), parts along dimension 0
There are 2 independent parts, one for each index of `groups`. A program takes and returns all parts, laid end to end along the dimension named above; an argument that names none is the same for every part. Nothing has to cross between parts.
Inputs may be any that keep to these rules, and one draw needn't show every extreme that they name: `expert_ids`: each row names two different experts. Among the rows of one device no expert is named more than 2 times, and in every draw some device names some expert exactly 2 times.
All inputs are finite; a program needn't handle non-finite values.
Results may differ from a plain program's by a relative error of at most 0.0081.
Values may be sent and summed in bfloat16 or wider, within the bound.
A program may use at most 128 MiB of HBM per device.

v0:
```python
import jax
import jax.numpy as jnp
from jax import lax
from jax.sharding import PartitionSpec as P

EXPERTS = 4
CAP = 2


def feed_forward(arrived_rows, gate_cols, up_cols, down_rows):
    layout = arrived_rows.shape
    flat_rows = arrived_rows.reshape(-1, layout[-1])
    gate_part = jnp.dot(flat_rows, gate_cols, preferred_element_type=jnp.float32)
    up_part = jnp.dot(flat_rows, up_cols, preferred_element_type=jnp.float32)
    hidden = (jax.nn.silu(gate_part) * up_part).astype(jnp.bfloat16)
    partial_value = jnp.dot(hidden, down_rows, preferred_element_type=jnp.float32)
    return partial_value.reshape(layout)


def send_back(partial_value):
    return lax.all_to_all(partial_value, "expert", split_axis=1, concat_axis=0, tiled=True)


def per_device(tokens, expert_ids, mix_weights, w_gate, w_up, w_down):
    shards = lax.axis_size("expert")
    owners = shards // EXPERTS
    tok_rows = tokens.shape[0]
    model_dim = tokens.shape[1]
    expert_range = jnp.arange(EXPERTS, dtype=jnp.int32)
    slot_count = EXPERTS * CAP
    flat_ids = expert_ids.reshape(-1)
    onehot = (flat_ids[:, None] == expert_range[None, :]).astype(jnp.int32)
    earlier = jnp.cumsum(onehot, axis=0) - onehot
    position = flat_ids * CAP + jnp.sum(earlier * onehot, axis=1)
    slot_map = (position[:, None] == jnp.arange(slot_count, dtype=jnp.int32)[None, :]).astype(
        jnp.float32
    )
    slot_map = slot_map.reshape(tok_rows, 2, slot_count)
    token_map = jnp.sum(slot_map, axis=1)
    combine = jnp.sum(slot_map * mix_weights[:, :, None], axis=1)
    compact = jnp.dot(
        token_map.T.astype(jnp.bfloat16), tokens, preferred_element_type=jnp.float32
    ).astype(jnp.bfloat16)
    outgoing = jnp.broadcast_to(
        compact.reshape(EXPERTS, 1, CAP, model_dim), (EXPERTS, owners, CAP, model_dim)
    )
    outgoing = outgoing.reshape(shards, 1, CAP, model_dim)
    paired = lax.all_gather(
        lax.all_to_all(outgoing, "expert", split_axis=0, concat_axis=1, tiled=True),
        "mp",
        axis=0,
        tiled=True,
    )
    partial_value = feed_forward(paired, w_gate, w_up, w_down)
    own_rows = lax.psum_scatter(partial_value, "mp", scatter_dimension=0, tiled=True)
    returned = send_back(own_rows)
    per_expert = jnp.sum(returned.reshape(EXPERTS, owners, CAP, model_dim), axis=1).reshape(
        slot_count, model_dim
    )
    combined = jnp.dot(
        combine, per_expert, precision=lax.Precision.HIGHEST, preferred_element_type=jnp.float32
    )
    return combined.astype(jnp.bfloat16)


def solution(mesh):
    in_specs = (
        P(("groups", "expert", "mp"), None),
        P(("groups", "expert", "mp"), None),
        P(("groups", "expert", "mp"), None),
        P(None, ("expert", "mp")),
        P(None, ("expert", "mp")),
        P(("expert", "mp"), None),
    )
    out_specs = P(("groups", "expert", "mp"), None)
    return jax.shard_map(
        per_device, mesh=mesh, in_specs=in_specs, out_specs=out_specs, check_vma=False
    )
```

profile of v0, /device:TPU:0, one launch (start us, length us, event | category | flops | bytes accessed | tf_op | source)
XLA Modules:
  0.0 93.4 jit_solution(9660064105527126358)
XLA Ops:
  6.5 0.0 copy-start
  6.5 0.8 eq.29
  7.3 0.1 fusion.8
  7.4 0.2 select_reduce_fusion.1
  7.6 0.1 reduce_sum.39
  7.7 0.7 multiply_add_fusion
  8.4 0.8 convert_reduce_fusion
  9.2 0.2 convolution_convert_fusion
  9.4 0.1 broadcast_in_dim.4
  9.5 0.1 broadcast_in_dim.5
  9.6 15.0 %all_to_all.21 = bf16[8,1,2,6144]{3,2,1,0:T(2,128)(2,1)S(1)} all-to-all(bf16[8,1,2,6144]{3,2,1,0:T(2,128)(2,1)S(1)} %bitcast.12), channel_id=1, replica_groups=mesh['groups'=2,'expert'=8,'mp'=2] {'expert'}, dimensions={0} | all-to-all | bytes 393216 | tf_op jit(solution)/shard_map/all_to_all | solution.py:49
  24.6 2.1 %all-gather = bf16[16,1,2,6144]{3,2,1,0:T(2,128)(2,1)S(1)} all-gather(bf16[8,1,2,6144]{3,2,1,0:T(2,128)(2,1)S(1)} %all_to_all.21), channel_id=2, replica_groups=mesh['groups'=2,'expert'=8,'mp'=2] {'mp'}, dimensions={0}, use_global_device_ids=true | all-gather | bytes 589824 | tf_op jit(solution)/shard_map/all_gather | solution.py:48
  26.7 0.1 reshape.45
  26.8 10.4 %fusion.11 = f32[32,2048]{1,0:T(8,128)S(1)} fusion(bf16[32,6144]{1,0:T(8,128)(2,1)S(1)} %reshape.45, bf16[6144,2048]{1,0:T(8,128)(2,1)} %param.9), kind=kOutput, calls=%fused_computation.20 | convolution fusion | flops 805306368 | bytes 25821184 | tf_op jit(solution)/shard_map/dot_general | solution.py:13
  37.3 19.8 %fusion.1 = f32[32,6144]{1,0:T(8,128)S(1)} fusion(bf16[2048,6144]{1,0:T(8,128)(2,1)} %param.11, bf16[32,6144]{1,0:T(8,128)(2,1)S(1)} %reshape.45, bf16[6144,2048]{1,0:T(8,128)(2,1)} %param.10, f32[32,2048]{1,0:T(8,128)S(1)} %fusion.11), kind=kOutput, calls=%fused_computation.4 | convolution fusion | flops 1611005952 | bytes 51773440 | tf_op jit(solution)/shard_map/dot_general | solution.py:16
  57.1 0.5 reshape.46
  57.6 1.3 %copy.9 = f32[2,8,2,6144]{3,1,2,0:T(8,128)} copy(f32[2,8,2,6144]{3,2,1,0:T(2,128)S(1)} %reshape.46) | data formatting | bytes 1572864 | tf_op jit(solution)/shard_map/reshape | solution.py:17
  58.9 0.0 reduce-scatter.2.cloned.1.call-update
  58.9 6.9 %reduce-scatter.2.cloned.1.call-done = f32[1,8,2,6144]{3,1,2,0:T(8,128)} async-done(((f32[2,8,2,6144]{3,1,2,0:T(8,128)}), f32[1,8,2,6144]{3,1,2,0:T(8,128)}) %reduce-scatter.2.cloned.1.call-update) | async-done | bytes 393232 | tf_op jit(solution)/shard_map/reduce_scatter | solution.py:55
  65.8 1.3 %copy.10 = f32[1,8,2,6144]{3,2,0,1:T(2,128)S(1)} copy(f32[1,8,2,6144]{3,1,2,0:T(8,128)} %reduce-scatter.2.cloned.1.call-done) | data formatting | bytes 786432 | tf_op jit(solution)/shard_map/reduce_scatter | solution.py:55
  67.2 18.1 %all_to_all.22 = f32[1,8,2,6144]{3,2,0,1:T(2,128)S(1)} all-to-all(f32[1,8,2,6144]{3,2,0,1:T(2,128)S(1)} %copy.10), channel_id=1, replica_groups=mesh['groups'=2,'expert'=8,'mp'=2] {'expert'}, dimensions={1} | all-to-all | bytes 786432 | tf_op jit(solution)/shard_map/all_to_all | solution.py:21
  85.2 0.3 reduce_sum.42
  85.5 0.1 reshape.48
  85.7 0.9 convolution_convert_fusion.1
  (3 shorter events, 0.0 us)
Async XLA Ops:
  6.5 2.6 %copy-start = (bf16[2,6144]{1,0:T(2,128)(2,1)S(1)}, bf16[2,6144]{1,0:T(2,128)(2,1)}, u32[]{:S(2)}) copy-start(bf16[2,6144]{1,0:T(2,128)(2,1)} %param.6) | copy-start | bytes 73732
  6.5 59.3 %reduce-scatter.2.cloned.1.call-start = ((), (), s32[]{:S(2)}) async-start(), calls=%async_computation.3 | async-start | bytes 1179648 | tf_op jit(solution)/shard_map/reduce_scatter | solution.py:55
Sparse Core Ops, SparseCore 0:
  59.1 6.7 reduce-scatter.1
where the time goes:
time: 93.8 us; the launch traced here: 93.4 us
  blocking collectives  35.2 us (38%)
  matrix products  31.4 us (33%)
  between operations  13.4 us (14%)
  waiting for transfers between devices  6.93 us (7%)
  local copies, waits for them, and re-layouts  4.43 us (5%)
  other arithmetic  2.04 us (2%)
    dot_general x1, matrix products, feed_forward(): jnp.dot(hidden, down_rows, preferred_element_type=jnp.float32)  19.8 us
    all_to_all x1, blocking collectives, send_back(): lax.all_to_all(partial_value, 'expert', split_axis=1, concat_axis=0, tile...  18.1 us
    all_to_all x1, blocking collectives, per_device(): lax.all_to_all(outgoing, 'expert', split_axis=0, concat_axis=1, tiled=True)  15 us
    dot_general x1, matrix products, feed_forward(): jnp.dot(flat_rows, gate_cols, preferred_element_type=jnp.float32)  10.4 us
    reduce_scatter x1, waiting for transfers between devices, per_device(): lax.psum_scatter(partial_value, 'mp', scatter_dimension=0, tiled=True)  6.92 us
    all_gather x1, blocking collectives, per_device(): lax.all_gather(lax.all_to_all(outgoing, 'expert', split_axis=0, concat_ax...  2.08 us
  transfers between devices with their start and end apart: 1, of which 1 were waited for; matrix products, arithmetic and copies ran while one was open for 0% of the time, Pallas kernels for 0%

commit v1 on v0

--- a/solution.py
+++ b/solution.py
@@ -18,7 +18,12 @@
 
 
 def send_back(partial_value):
-    return lax.all_to_all(partial_value, "expert", split_axis=1, concat_axis=0, tiled=True)
+    return jnp.concatenate(
+        lax.all_to_all(
+            jnp.stack(jnp.split(partial_value, lax.axis_size("expert"), axis=1)), "expert", 0, 0
+        ),
+        axis=0,
+    )
 
 
 def per_device(tokens, expert_ids, mix_weights, w_gate, w_up, w_down):

time: 93.8 us -> 101 us (1.077)
  local copies, waits for them, and re-layouts: 4.43 us -> 11.7 us
    unnamed x2 -> x10, local copies, waits for them, and re-layouts: 0.01 us -> 7.52 us
    reduce_scatter x1 -> x0, local copies, waits for them, and re-layouts: 1.3 us -> none  [per_device(): lax.psum_scatter(partial_value, 'mp', scatter_dimension=0, tiled=True)]
    another operation x0 -> x1, local copies, waits for them, and re-layouts: none -> 1.05 us  [send_back(): jnp.stack(jnp.split(partial_value, lax.axis_size('expert'), axis=1))]
where the time goes in v1:
time: 101 us
  blocking collectives  35.2 us (35%)
  matrix products  31.4 us (31%)
  between operations  13.5 us (13%)
  local copies, waits for them, and re-layouts  11.7 us (12%)
  waiting for transfers between devices  6.93 us (7%)
  other arithmetic  2.05 us (2%)
    dot_general x1, matrix products, feed_forward(): jnp.dot(hidden, down_rows, preferred_element_type=jnp.float32)  19.8 us
    all_to_all x1, blocking collectives, send_back(): lax.all_to_all(jnp.stack(jnp.split(partial_value, lax.axis_size('expert')...  18.1 us
    all_to_all x1, blocking collectives, per_device(): lax.all_to_all(outgoing, 'expert', split_axis=0, concat_axis=1, tiled=True)  15 us
    dot_general x1, matrix products, feed_forward(): jnp.dot(flat_rows, gate_cols, preferred_element_type=jnp.float32)  10.4 us
    unnamed x10, local copies, waits for them, and re-layouts  7.52 us
    reduce_scatter x1, waiting for transfers between devices, per_device(): lax.psum_scatter(partial_value, 'mp', scatter_dimension=0, tiled=True)  6.92 us
    all_gather x1, blocking collectives, per_device(): lax.all_gather(lax.all_to_all(outgoing, 'expert', split_axis=0, concat_ax...  2.08 us
  transfers between devices with their start and end apart: 1, of which 1 were waited for; matrix products, arithmetic and copies ran while one was open for 0% of the time, Pallas kernels for 0%

profile of v1, /device:TPU:0, one launch (start us, length us, event | category | flops | bytes accessed | tf_op | source)
XLA Modules:
  0.0 100.7 jit_solution(10418546287056508496)
XLA Ops:
  6.5 0.8 eq.29
  7.4 0.2 select_reduce_fusion.1
  7.7 0.7 multiply_add_fusion
  8.4 0.8 convert_reduce_fusion
  9.2 0.2 convolution_convert_fusion
  9.6 15.0 %all_to_all.17 = bf16[8,1,2,6144]{3,2,1,0:T(2,128)(2,1)S(1)} all-to-all(bf16[8,1,2,6144]{3,2,1,0:T(2,128)(2,1)S(1)} %bitcast.44), channel_id=1, replica_groups=mesh['groups'=2,'expert'=8,'mp'=2] {'expert'}, dimensions={0} | all-to-all | bytes 393216 | tf_op jit(solution)/shard_map/all_to_all | solution.py:54
  24.6 2.1 %all-gather = bf16[16,1,2,6144]{3,2,1,0:T(2,128)(2,1)S(1)} all-gather(bf16[8,1,2,6144]{3,2,1,0:T(2,128)(2,1)S(1)} %all_to_all.17), channel_id=2, replica_groups=mesh['groups'=2,'expert'=8,'mp'=2] {'mp'}, dimensions={0}, use_global_device_ids=true | all-gather | bytes 589824 | tf_op jit(solution)/shard_map/all_gather | solution.py:53
  26.8 10.4 %fusion.19 = f32[32,2048]{1,0:T(8,128)S(1)} fusion(bf16[32,6144]{1,0:T(8,128)(2,1)S(1)} %reshape.38, bf16[6144,2048]{1,0:T(8,128)(2,1)} %param.9), kind=kOutput, calls=%fused_computation.36 | convolution fusion | flops 805306368 | bytes 25821184 | tf_op jit(solution)/shard_map/dot_general | solution.py:13
  37.3 19.8 %fusion.1 = f32[32,6144]{1,0:T(8,128)S(1)} fusion(bf16[2048,6144]{1,0:T(8,128)(2,1)} %param.11, bf16[32,6144]{1,0:T(8,128)(2,1)S(1)} %reshape.38, bf16[6144,2048]{1,0:T(8,128)(2,1)} %param.10, f32[32,2048]{1,0:T(8,128)S(1)} %fusion.19), kind=kOutput, calls=%fused_computation.4 | convolution fusion | flops 1611005952 | bytes 51773440 | tf_op jit(solution)/shard_map/dot_general | solution.py:16
  57.1 0.5 reshape.39
  57.6 1.3 %copy.8 = f32[2,8,2,6144]{3,1,2,0:T(8,128)} copy(f32[2,8,2,6144]{3,2,1,0:T(2,128)S(1)} %reshape.39) | data formatting | bytes 1572864 | tf_op jit(solution)/shard_map/reshape | solution.py:17
  58.9 6.9 %reduce-scatter.2.cloned.1.call-done = f32[1,8,2,6144]{3,1,2,0:T(8,128)} async-done(((f32[2,8,2,6144]{3,1,2,0:T(8,128)}), f32[1,8,2,6144]{3,1,2,0:T(8,128)}) %reduce-scatter.2.cloned.1.call-update) | async-done | bytes 393232 | tf_op jit(solution)/shard_map/reduce_scatter | solution.py:60
  65.8 1.0 %fusion.15 = f32[8,1,1,2,6144]{4,1,3,2,0:T(1,128)S(1)} fusion(f32[1,8,2,6144]{3,1,2,0:T(8,128)} %reduce-scatter.2.cloned.1.call-done), kind=kLoop, calls=%fused_computation.26 | loop fusion | bytes 98304
  66.9 1.0 %fusion.14 = f32[8,1,1,2,6144]{4,1,3,2,0:T(1,128)S(1)} fusion(f32[8,1,1,2,6144]{4,1,3,2,0:T(1,128)S(1)} %fusion.15, f32[1,8,2,6144]{3,1,2,0:T(8,128)} %reduce-scatter.2.cloned.1.call-done), kind=kLoop, calls=%fused_computation.24 | loop fusion | bytes 98304
  67.9 1.0 %fusion.13 = f32[8,1,1,2,6144]{4,1,3,2,0:T(1,128)S(1)} fusion(f32[8,1,1,2,6144]{4,1,3,2,0:T(1,128)S(1)} %fusion.14, f32[1,8,2,6144]{3,1,2,0:T(8,128)} %reduce-scatter.2.cloned.1.call-done), kind=kLoop, calls=%fused_computation.22 | loop fusion | bytes 98304
  69.0 1.0 %fusion.12 = f32[8,1,1,2,6144]{4,1,3,2,0:T(1,128)S(1)} fusion(f32[8,1,1,2,6144]{4,1,3,2,0:T(1,128)S(1)} %fusion.13, f32[1,8,2,6144]{3,1,2,0:T(8,128)} %reduce-scatter.2.cloned.1.call-done), kind=kLoop, calls=%fused_computation.20 | loop fusion | bytes 98304
  70.0 1.0 %fusion.11 = f32[8,1,1,2,6144]{4,1,3,2,0:T(1,128)S(1)} fusion(f32[8,1,1,2,6144]{4,1,3,2,0:T(1,128)S(1)} %fusion.12, f32[1,8,2,6144]{3,1,2,0:T(8,128)} %reduce-scatter.2.cloned.1.call-done), kind=kLoop, calls=%fused_computation.18 | loop fusion | bytes 98304
  71.1 1.0 %fusion.10 = f32[8,1,1,2,6144]{4,1,3,2,0:T(1,128)S(1)} fusion(f32[8,1,1,2,6144]{4,1,3,2,0:T(1,128)S(1)} %fusion.11, f32[1,8,2,6144]{3,1,2,0:T(8,128)} %reduce-scatter.2.cloned.1.call-done), kind=kLoop, calls=%fused_computation.16 | loop fusion | bytes 98304
  72.1 1.0 %fusion.9 = f32[8,1,1,2,6144]{4,1,3,2,0:T(1,128)S(1)} fusion(f32[8,1,1,2,6144]{4,1,3,2,0:T(1,128)S(1)} %fusion.10, f32[1,8,2,6144]{3,1,2,0:T(8,128)} %reduce-scatter.2.cloned.1.call-done), kind=kLoop, calls=%fused_computation.14 | loop fusion | bytes 98304
  73.2 1.0 %fusion.8 = f32[8,1,1,2,6144]{4,1,3,2,0:T(1,128)S(1)} fusion(f32[8,1,1,2,6144]{4,1,3,2,0:T(1,128)S(1)} %fusion.9, f32[1,8,2,6144]{3,1,2,0:T(8,128)} %reduce-scatter.2.cloned.1.call-done), kind=kLoop, calls=%fused_computation.12 | loop fusion | bytes 98304 | tf_op jit(solution)/shard_map/stack | solution.py:23
  74.2 18.1 %all_to_all.18 = f32[8,1,1,2,6144]{4,1,3,2,0:T(1,128)S(1)} all-to-all(f32[8,1,1,2,6144]{4,1,3,2,0:T(1,128)S(1)} %fusion.8), channel_id=1, replica_groups=mesh['groups'=2,'expert'=8,'mp'=2] {'expert'}, dimensions={0} | all-to-all | bytes 786432 | tf_op jit(solution)/shard_map/all_to_all | solution.py:22
  92.3 0.2 copy.9
  92.5 0.3 reduce_sum.42
  92.9 0.9 convolution_convert_fusion.1
  (11 shorter events, 0.7 us)
Async XLA Ops:
  6.5 2.6 %copy-start = (bf16[2,6144]{1,0:T(2,128)(2,1)S(1)}, bf16[2,6144]{1,0:T(2,128)(2,1)}, u32[]{:S(2)}) copy-start(bf16[2,6144]{1,0:T(2,128)(2,1)} %param.6) | copy-start | bytes 73732
  6.5 59.3 %reduce-scatter.2.cloned.1.call-start = ((), (), s32[]{:S(2)}) async-start(), calls=%async_computation.3 | async-start | bytes 1179648 | tf_op jit(solution)/shard_map/reduce_scatter | solution.py:60
Sparse Core Ops, SparseCore 0:
  59.1 6.7 reduce-scatter.1
